TPU v7x, 32 devices: a whole 2x2x4 slice. The times are simulated.
32 devices in a mesh: freq: 2 (over x), leaf: 16 (over z, y, core).
Axes of the slice: x: 2, y: 2, z: 4, core: 2. Of those that a mesh axis runs over, the one named last changes fastest.
Arguments:
- rhs: float32 [128, 256, 128], P(('freq', 'leaf')), parts along dimension 0, may hold values from -6 to 6
- leaf_q: float32 [128, 256, 256], P(('freq', 'leaf')), parts along dimension 0, may hold values from -0.375 to 0.375
- leaf_e: float32 [128, 256, 256], P(('freq', 'leaf')), parts along dimension 0, may hold values from -0.375 to 0.375
- leaf_w: float32 [128, 256, 128], P(('freq', 'leaf')), parts along dimension 0, may hold values from -0.375 to 0.375
- node_q: float32 [96, 256, 256], P(('freq', 'leaf')), parts along dimension 0, may hold values from -0.375 to 0.375
- node_e: float32 [96, 256, 256], P(('freq', 'leaf')), parts along dimension 0, may hold values from -0.375 to 0.375
- node_w: float32 [96, 256, 128], P(('freq', 'leaf')), parts along dimension 0, may hold values from -0.375 to 0.375
- top_q: float32 [128, 256, 256], P(('freq', 'leaf')), parts along dimension 0, as said below
- top_e: float32 [128, 256, 256], P(('freq', 'leaf')), parts along dimension 0, as said below
- top_w: float32 [128, 256, 128], P(('freq', 'leaf')), parts along dimension 0, as said below
Outputs:
- solution: float32 [128, 256, 128], P(('freq', 'leaf')), parts along dimension 0
There are 2 independent parts, one for each index of `freq`. A program takes and returns all parts, laid end to end along the dimension named above; each array names one. Nothing has to cross between parts.
Inputs may be any that keep to these rules, and one draw needn't show every extreme that they name: Device d's 4 rows of top_q hold, in row l-1, the transform of the level l node d // 2^l; devices with equal d // 2^l hold equal rows l-1. `top_e`: likewise for the inverted blocks: row l-1 of device d belongs to node d // 2^l of level l and is equal on all devices of that node. `top_w`: likewise for the generators: row l-1 of device d belongs to node d // 2^l of level l and is equal on all devices of that node.
All inputs are finite; a program needn't handle non-finite values.
Results may differ from a plain program's by a relative error of at most 0.00012.
Values sent between devices are 32-bit elements; how exact they have to be, the bound alone decides.
A program may use at most 64 MiB of HBM per device.

v0:
```python
import jax
import jax.numpy as jnp
from jax import lax
from jax.sharding import PartitionSpec as P

HIGH = lax.Precision.HIGHEST


def swapped(value, axis, apart):
    mask = 2**apart
    pairs = [(source, source ^ mask) for source in range(lax.axis_size(axis))]
    return lax.ppermute(value, axis, pairs)


def batched(mats, vecs):
    return jnp.einsum("nij,njr->nir", mats, vecs, precision=HIGH)


def batched_t(mats, vecs):
    return jnp.einsum("nji,njr->nir", mats, vecs, precision=HIGH)


def upward(qmat, emat, wmat, vecs):
    values = batched(emat, batched(qmat, vecs))
    return (values, batched_t(wmat, values))


def downward(qmat, emat, wmat, values, parent):
    return batched_t(qmat, values - batched(emat, batched(wmat, parent)))


def pick_level(gens, level, leaf_count):
    count = leaf_count // 2**level
    offset = leaf_count - 2 * count
    return gens[offset : offset + count]


def tree_sweep(reduced, top_q, top_e, top_w, width):
    parts = lax.axis_size("leaf")
    position = lax.axis_index("leaf")
    levels = parts.bit_length() - 1
    upper_values = []
    for level in range(1, levels + 1):
        other = swapped(reduced, "leaf", level - 1)
        on_right = position // 2 ** (level - 1) % 2 == 1
        stacked = jnp.where(
            on_right,
            jnp.concatenate([other, reduced], axis=1),
            jnp.concatenate([reduced, other], axis=1),
        )
        values, reduced = upward(
            top_q[level - 1 : level], top_e[level - 1 : level], top_w[level - 1 : level], stacked
        )
        upper_values.append(values)
    answer = upper_values[-1]
    parent = answer[:, :width]
    for level in range(levels, 0, -1):
        on_right = position // 2 ** (level - 1) % 2 == 1
        parent = jnp.where(on_right, answer[:, width:], answer[:, :width])
        if level > 1:
            answer = downward(
                top_q[level - 2 : level - 1],
                top_e[level - 2 : level - 1],
                top_w[level - 2 : level - 1],
                upper_values[level - 2],
                parent,
            )
    return parent


def body(rhs, leaf_q, leaf_e, leaf_w, node_q, node_e, node_w, top_q, top_e, top_w):
    width = leaf_w.shape[2]
    cols = rhs.shape[2]
    leaf_count = rhs.shape[0]
    local_levels = leaf_count.bit_length() - 1
    values, reduced = upward(leaf_q, leaf_e, leaf_w, rhs)
    local_values = [values]
    for level in range(1, local_levels + 1):
        stacked = reduced.reshape(-1, 2 * width, cols)
        values, reduced = upward(
            pick_level(node_q, level, leaf_count),
            pick_level(node_e, level, leaf_count),
            pick_level(node_w, level, leaf_count),
            stacked,
        )
        local_values.append(values)
    half = cols // 2
    first = tree_sweep(reduced[:, :, :half], top_q, top_e, top_w, width)
    second = tree_sweep(reduced[:, :, half:], top_q, top_e, top_w, width)
    parent = jnp.concatenate([first, second], axis=2)
    for level in range(local_levels, 0, -1):
        answer = downward(
            pick_level(node_q, level, leaf_count),
            pick_level(node_e, level, leaf_count),
            pick_level(node_w, level, leaf_count),
            local_values[level],
            parent,
        )
        parent = answer.reshape(-1, width, cols)
    return downward(leaf_q, leaf_e, leaf_w, local_values[0], parent)


def solution(mesh):
    in_specs = (
        P(("freq", "leaf"), None, None),
        P(("freq", "leaf"), None, None),
        P(("freq", "leaf"), None, None),
        P(("freq", "leaf"), None, None),
        P(("freq", "leaf"), None, None),
        P(("freq", "leaf"), None, None),
        P(("freq", "leaf"), None, None),
        P(("freq", "leaf"), None, None),
        P(("freq", "leaf"), None, None),
        P(("freq", "leaf"), None, None),
    )
    out_specs = P(("freq", "leaf"), None, None)
    return jax.shard_map(body, mesh=mesh, in_specs=in_specs, out_specs=out_specs, check_vma=False)
```

profile of v0, /device:TPU:0, one launch (start us, length us, event | category | flops | bytes accessed | tf_op | source)
XLA Modules:
  0.0 45.8 jit_solution(10212250054275632589)
XLA Ops:
  0.0 2.7 %fusion.218 = f32[4,256,128]{1,2,0:T(8,128)S(1)} fusion(f32[4,256,256]{2,1,0:T(8,128)} %param.11, f32[4,256,128]{2,1,0:T(8,128)} %param.10), kind=kOutput, calls=%fused_computation.253 | convolution fusion | flops 402653184 | bytes 2097152 | tf_op jit(solution)/shard_map/nij,njr->nir/dot_general | solution.py:16
  2.7 1.2 %fusion.219 = f32[4,128,256]{2,1,0:T(8,128)S(1)} fusion(f32[4,256,128]{1,2,0:T(8,128)S(1)} %fusion.218, f32[4,256,256]{2,1,0:T(8,128)S(1)} %copy-done), kind=kOutput, calls=%fused_computation.254 | convolution fusion | flops 402653184 | bytes 2097152 | tf_op jit(solution)/shard_map/nij,njr->nir/dot_general | solution.py:16
  3.9 1.0 %fusion.220 = f32[4,128,128]{1,2,0:T(8,128)S(1)} fusion(f32[4,128,256]{2,1,0:T(8,128)S(1)} %fusion.219, f32[4,256,128]{2,1,0:T(8,128)S(1)} %copy-done.11), kind=kOutput, calls=%fused_computation.255 | convolution fusion | flops 201326592 | bytes 1310720 | tf_op jit(solution)/shard_map/nji,njr->nir/dot_general | solution.py:20
  5.2 0.7 %fusion.5 = f32[2,128,256]{2,1,0:T(8,128)S(1)} fusion(f32[2,256,128]{2,1,0:T(8,128)S(1)} %bitcast.265, f32[3,256,256]{2,1,0:T(8,128)S(1)} %copy-done.9), kind=kOutput, calls=%fused_computation.25 | convolution fusion | flops 201326592 | bytes 1048576 | tf_op jit(solution)/shard_map/nij,njr->nir/dot_general | solution.py:16
  6.2 0.6 %fusion.2 = f32[2,128,256]{2,1,0:T(8,128)S(1)} fusion(f32[2,128,256]{2,1,0:T(8,128)S(1)} %fusion.5, f32[3,256,256]{2,1,0:T(8,128)S(1)} %copy-done.7), kind=kOutput, calls=%fused_computation.22 | convolution fusion | flops 201326592 | bytes 1048576 | tf_op jit(solution)/shard_map/nij,njr->nir/dot_general | solution.py:16
  7.2 0.6 %fusion.64 = f32[2,128,128]{1,2,0:T(8,128)S(1)} fusion(f32[2,128,256]{2,1,0:T(8,128)S(1)} %fusion.2, f32[3,256,128]{2,1,0:T(8,128)S(1)} %copy-done.13), kind=kOutput, calls=%fused_computation.85 | convolution fusion | flops 100663296 | bytes 655360 | tf_op jit(solution)/shard_map/nji,njr->nir/dot_general | solution.py:20
  8.9 0.7 %fusion.217 = (f32[1,128,64]{1,2,0:T(8,128)}, f32[128,64]{0,1:T(8,128)}, f32[128,64]{0,1:T(8,128)}, f32[1,128,64]{1,2,0:T(8,128)}) fusion(f32[1,128,128]{1,2,0:T(8,128)S(1)} %convolution_bitcast_fusion.10), kind=kLoop, calls=%fused_computation.252 | loop fusion | bytes 196608 | tf_op jit(solution)/shard_map/slice | solution.py:88
  10.1 1.2 %collective-permute-done = f32[1,128,64]{1,2,0:T(8,128)} collective-permute-done((f32[1,128,64]{1,2,0:T(8,128)}, f32[1,128,64]{1,2,0:T(8,128)}, u32[]{:S(2)}, u32[]{:S(2)}) %collective-permute-start) | collective-permute-done | bytes 32800 | tf_op jit(solution)/shard_map/ppermute | solution.py:12
  11.3 1.2 %fusion.50 = f32[64,256]{1,0:T(8,128)S(1)} fusion(f32[4,256,256]{2,1,0:T(8,128)S(1)} %copy-done.2, f32[128,64]{0,1:T(8,128)} %get-tuple-element.6, f32[128,64]{0,1:T(8,128)} %bitcast.9, pred[]{:T(512)S(6)} %eq.41), kind=kOutput, calls=%fused_computation.70 | convolution fusion | flops 50380800 | bytes 393217 | tf_op jit(solution)/shard_map/nij,njr->nir/dot_general | solution.py:16
  13.1 2.9 %collective-permute-start.1 = (f32[1,128,64]{1,2,0:T(8,128)S(1)}, f32[1,128,64]{1,2,0:T(8,128)S(1)}, u32[]{:S(2)}, u32[]{:S(2)}) collective-permute-start(f32[1,128,64]{1,2,0:T(8,128)S(1)} %bitcast.270), channel_id=1, source_target_pairs={{0,2},{1,3},{2,0},{3,1},{4,6},{5,7},{6,4},{7,5},{8,10},{9,11},{10,... | collective-permute-start | bytes 98312 | tf_op jit(solution)/shard_map/ppermute | solution.py:12
  16.0 1.2 %fusion.47 = f32[64,256]{1,0:T(8,128)S(1)} fusion(f32[4,256,256]{2,1,0:T(8,128)S(1)} %copy-done.2, f32[128,64]{0,1:T(8,128)S(1)} %copy-done.15, f32[128,64]{0,1:T(8,128)} %bitcast.47, pred[]{:T(512)S(6)} %eq.41), kind=kOutput, calls=%fused_computation.67 | convolution fusion | flops 50380800 | bytes 393217 | tf_op jit(solution)/shard_map/nij,njr->nir/dot_general | solution.py:16
  17.8 0.5 %collective-permute-start.5 = (f32[1,128,64]{1,2,0:T(8,128)S(1)}, f32[1,128,64]{1,2,0:T(8,128)S(1)}, u32[]{:S(2)}, u32[]{:S(2)}) collective-permute-start(f32[1,128,64]{1,2,0:T(8,128)S(1)} %bitcast.272), channel_id=1, source_target_pairs={{0,2},{1,3},{2,0},{3,1},{4,6},{5,7},{6,4},{7,5},{8,10},{9,11},{10,... | collective-permute-start | bytes 98312 | tf_op jit(solution)/shard_map/ppermute | solution.py:12
  19.3 1.7 %collective-permute-start.2 = (f32[1,128,64]{1,2,0:T(8,128)S(1)}, f32[1,128,64]{1,2,0:T(8,128)S(1)}, u32[]{:S(2)}, u32[]{:S(2)}) collective-permute-start(f32[1,128,64]{1,2,0:T(8,128)S(1)} %bitcast.274), channel_id=1, source_target_pairs={{0,4},{1,5},{2,6},{3,7},{4,0},{5,1},{6,2},{7,3},{8,12},{9,13},{10,... | collective-permute-start | bytes 98312 | tf_op jit(solution)/shard_map/ppermute | solution.py:12
  21.0 0.8 %collective-permute-done.5 = f32[1,128,64]{1,2,0:T(8,128)S(1)} collective-permute-done((f32[1,128,64]{1,2,0:T(8,128)S(1)}, f32[1,128,64]{1,2,0:T(8,128)S(1)}, u32[]{:S(2)}, u32[]{:S(2)}) %collective-permute-start.5) | collective-permute-done | bytes 32800 | tf_op jit(solution)/shard_map/ppermute | solution.py:12
  22.8 1.6 %collective-permute-start.6 = (f32[1,128,64]{1,2,0:T(8,128)S(1)}, f32[1,128,64]{1,2,0:T(8,128)S(1)}, u32[]{:S(2)}, u32[]{:S(2)}) collective-permute-start(f32[1,128,64]{1,2,0:T(8,128)S(1)} %bitcast.276), channel_id=1, source_target_pairs={{0,4},{1,5},{2,6},{3,7},{4,0},{5,1},{6,2},{7,3},{8,12},{9,13},{10,... | collective-permute-start | bytes 98312 | tf_op jit(solution)/shard_map/ppermute | solution.py:12
  25.4 2.7 %collective-permute-start.3 = (f32[1,128,64]{1,2,0:T(8,128)S(1)}, f32[1,128,64]{1,2,0:T(8,128)S(1)}, u32[]{:S(2)}, u32[]{:S(2)}) collective-permute-start(f32[1,128,64]{1,2,0:T(8,128)S(1)} %bitcast.278), channel_id=1, source_target_pairs={{0,8},{1,9},{2,10},{3,11},{4,12},{5,13},{6,14},{7,15},{8,0},{9,1},... | collective-permute-start | bytes 98312 | tf_op jit(solution)/shard_map/ppermute | solution.py:12
  29.0 1.4 %collective-permute-start.7 = (f32[1,128,64]{1,2,0:T(8,128)S(1)}, f32[1,128,64]{1,2,0:T(8,128)S(1)}, u32[]{:S(2)}, u32[]{:S(2)}) collective-permute-start(f32[1,128,64]{1,2,0:T(8,128)S(1)} %bitcast.268), channel_id=1, source_target_pairs={{0,8},{1,9},{2,10},{3,11},{4,12},{5,13},{6,14},{7,15},{8,0},{9,1},... | collective-permute-start | bytes 98312 | tf_op jit(solution)/shard_map/ppermute | solution.py:12
  34.2 0.5 %fusion.12 = f32[64,256]{1,0:T(8,128)S(1)} fusion(f32[4,256,256]{2,1,0:T(8,128)S(1)} %copy-done.2, f32[128,64]{0,1:T(8,128)S(1)} %bitcast.269, f32[128,64]{0,1:T(8,128)S(1)} %bitcast.280, pred[]{:T(512)S(6)} %eq.44), kind=kOutput, calls=%fused_computation.32 | convolution fusion | flops 50380800 | bytes 393217 | tf_op jit(solution)/shard_map/nij,njr->nir/dot_general | solution.py:16
  39.7 0.6 %convolution_subtract_fusion.1 = f32[2,128,256]{2,1,0:T(8,128)S(1)} fusion(f32[2,128,256]{2,1,0:T(8,128)S(1)} %fusion.2, f32[2,128,256]{2,1,0:T(8,128)S(1)} %fusion.66, f32[3,256,256]{2,1,0:T(8,128)S(1)} %copy-done.8), kind=kOutput, calls=%fused_computation.3 | convolution fusion | flops 201392128 | bytes 1310720 | tf_op jit(solution)/shard_map/nij,njr->nir/dot_general | solution.py:16
  40.9 0.9 %copy-done.12 = f32[4,256,128]{2,1,0:T(8,128)S(1)} copy-done((f32[4,256,128]{2,1,0:T(8,128)S(1)}, f32[4,256,128]{2,1,0:T(8,128)}, u32[]{:S(2)}) %copy-start.12) | copy-done | bytes 524312
  41.8 0.6 %fusion.221 = f32[4,128,256]{2,1,0:T(8,128)S(1)} fusion(f32[4,128,128]{2,1,0:T(8,128)S(1)} %bitcast.264, f32[4,256,128]{2,1,0:T(8,128)S(1)} %copy-done.12), kind=kOutput, calls=%fused_computation.256 | convolution fusion | flops 201326592 | bytes 1310720 | tf_op jit(solution)/shard_map/nij,njr->nir/dot_general | solution.py:16
  42.9 1.2 %convolution_subtract_fusion = f32[4,128,256]{2,1,0:T(8,128)S(1)} fusion(f32[4,128,256]{2,1,0:T(8,128)S(1)} %copy-done.5, f32[4,128,256]{2,1,0:T(8,128)S(1)} %fusion.221, f32[4,256,256]{2,1,0:T(8,128)S(1)} %copy-done), kind=kOutput, calls=%fused_computation | convolution fusion | flops 402784256 | bytes 2621440 | tf_op jit(solution)/shard_map/nij,njr->nir/dot_general | solution.py:16
  44.1 0.8 %convolution_bitcast_fusion = f32[4,256,128]{1,2,0:T(8,128)S(1)} fusion(f32[4,128,256]{2,1,0:T(8,128)S(1)} %convolution_subtract_fusion, f32[4,256,256]{2,1,0:T(8,128)S(1)} %copy-done.6), kind=kOutput, calls=%fused_computation.1 | convolution fusion | flops 402653184 | bytes 2097152 | tf_op jit(solution)/shard_map/nji,njr->nir/dot_general | solution.py:20
  44.8 1.0 %copy.17 = f32[4,256,128]{2,1,0:T(8,128)} copy(f32[4,256,128]{1,2,0:T(8,128)S(1)} %convolution_bitcast_fusion) | data formatting | bytes 1048576 | tf_op jit(solution)/shard_map/nji,njr->nir/dot_general | solution.py:20
  (87 shorter events, 17.1 us)
Async XLA Ops:
  0.0 2.7 %copy-start = (f32[4,256,256]{2,1,0:T(8,128)S(1)}, f32[4,256,256]{2,1,0:T(8,128)}, u32[]{:S(2)}) copy-start(f32[4,256,256]{2,1,0:T(8,128)} %param.12) | copy-start | bytes 3145732
  2.7 1.2 %copy-start.11 = (f32[4,256,128]{2,1,0:T(8,128)S(1)}, f32[4,256,128]{2,1,0:T(8,128)}, u32[]{:S(2)}) copy-start(f32[4,256,128]{2,1,0:T(8,128)} %param.13) | copy-start | bytes 1572868
  3.9 1.1 %copy-start.4 = (f32[4,128,256]{2,1,0:T(8,128)}, f32[4,128,256]{2,1,0:T(8,128)S(1)}, u32[]{:S(2)}) copy-start(f32[4,128,256]{2,1,0:T(8,128)S(1)} %fusion.219) | copy-start | bytes 1572868
  3.9 1.3 %copy-start.9 = (f32[3,256,256]{2,1,0:T(8,128)S(1)}, f32[3,256,256]{2,1,0:T(8,128)}, u32[]{:S(2)}) copy-start(f32[3,256,256]{2,1,0:T(8,128)} %param.14) | copy-start | bytes 2359300
  5.0 1.2 %copy-start.7 = (f32[3,256,256]{2,1,0:T(8,128)S(1)}, f32[3,256,256]{2,1,0:T(8,128)}, u32[]{:S(2)}) copy-start(f32[3,256,256]{2,1,0:T(8,128)} %param.15) | copy-start | bytes 2359300
  6.2 1.0 %copy-start.13 = (f32[3,256,128]{2,1,0:T(8,128)S(1)}, f32[3,256,128]{2,1,0:T(8,128)}, u32[]{:S(2)}) copy-start(f32[3,256,128]{2,1,0:T(8,128)} %param.16) | copy-start | bytes 1179652
  7.2 4.1 %copy-start.2 = (f32[4,256,256]{2,1,0:T(8,128)S(1)}, f32[4,256,256]{2,1,0:T(8,128)}, u32[]{:S(2)}) copy-start(f32[4,256,256]{2,1,0:T(8,128)} %param.17) | copy-start | bytes 3145732
  7.8 4.7 %copy-start.1 = (f32[4,256,256]{2,1,0:T(8,128)S(1)}, f32[4,256,256]{2,1,0:T(8,128)}, u32[]{:S(2)}) copy-start(f32[4,256,256]{2,1,0:T(8,128)} %param.18) | copy-start | bytes 3145732
  9.6 1.7 %collective-permute-start = (f32[1,128,64]{1,2,0:T(8,128)}, f32[1,128,64]{1,2,0:T(8,128)}, u32[]{:S(2)}, u32[]{:S(2)}) collective-permute-start(f32[1,128,64]{1,2,0:T(8,128)} %get-tuple-element.5), channel_id=1, source_target_pairs={{0,1},{1,0},{2,3},{3,2},{4,5},{5,4},{6,7},{7,6},{8,9},{9,8},{10,11... | collective-permute-start | bytes 98312 | tf_op jit(solution)/shard_map/ppermute | solution.py:12
  10.1 5.9 %collective-permute-start.4 = (f32[1,128,64]{1,2,0:T(8,128)}, f32[1,128,64]{1,2,0:T(8,128)}, u32[]{:S(2)}, u32[]{:S(2)}) collective-permute-start(f32[1,128,64]{1,2,0:T(8,128)} %get-tuple-element.8), channel_id=1, source_target_pairs={{0,1},{1,0},{2,3},{3,2},{4,5},{5,4},{6,7},{7,6},{8,9},{9,8},{10,11... | collective-permute-start | bytes 98312 | tf_op jit(solution)/shard_map/ppermute | solution.py:12
  10.1 2.8 %copy-start.3 = (f32[4,256,128]{2,1,0:T(8,128)S(1)}, f32[4,256,128]{2,1,0:T(8,128)}, u32[]{:S(2)}) copy-start(f32[4,256,128]{2,1,0:T(8,128)} %param.19) | copy-start | bytes 1572868
  12.9 3.2 %copy-start.15 = (f32[128,64]{0,1:T(8,128)S(1)}, f32[128,64]{0,1:T(8,128)}, u32[]{:S(2)}) copy-start(f32[128,64]{0,1:T(8,128)} %get-tuple-element.7) | copy-start | bytes 98308
  13.1 5.2 %collective-permute-start.1 = (f32[1,128,64]{1,2,0:T(8,128)S(1)}, f32[1,128,64]{1,2,0:T(8,128)S(1)}, u32[]{:S(2)}, u32[]{:S(2)}) collective-permute-start(f32[1,128,64]{1,2,0:T(8,128)S(1)} %bitcast.270), channel_id=1, source_target_pairs={{0,2},{1,3},{2,0},{3,1},{4,6},{5,7},{6,4},{7,5},{8,10},{9,11},{10,... | collective-permute-start | bytes 98312 | tf_op jit(solution)/shard_map/ppermute | solution.py:12
  17.8 4.0 %collective-permute-start.5 = (f32[1,128,64]{1,2,0:T(8,128)S(1)}, f32[1,128,64]{1,2,0:T(8,128)S(1)}, u32[]{:S(2)}, u32[]{:S(2)}) collective-permute-start(f32[1,128,64]{1,2,0:T(8,128)S(1)} %bitcast.272), channel_id=1, source_target_pairs={{0,2},{1,3},{2,0},{3,1},{4,6},{5,7},{6,4},{7,5},{8,10},{9,11},{10,... | collective-permute-start | bytes 98312 | tf_op jit(solution)/shard_map/ppermute | solution.py:12
  19.3 5.1 %collective-permute-start.2 = (f32[1,128,64]{1,2,0:T(8,128)S(1)}, f32[1,128,64]{1,2,0:T(8,128)S(1)}, u32[]{:S(2)}, u32[]{:S(2)}) collective-permute-start(f32[1,128,64]{1,2,0:T(8,128)S(1)} %bitcast.274), channel_id=1, source_target_pairs={{0,4},{1,5},{2,6},{3,7},{4,0},{5,1},{6,2},{7,3},{8,12},{9,13},{10,... | collective-permute-start | bytes 98312 | tf_op jit(solution)/shard_map/ppermute | solution.py:12
  22.8 5.3 %collective-permute-start.6 = (f32[1,128,64]{1,2,0:T(8,128)S(1)}, f32[1,128,64]{1,2,0:T(8,128)S(1)}, u32[]{:S(2)}, u32[]{:S(2)}) collective-permute-start(f32[1,128,64]{1,2,0:T(8,128)S(1)} %bitcast.276), channel_id=1, source_target_pairs={{0,4},{1,5},{2,6},{3,7},{4,0},{5,1},{6,2},{7,3},{8,12},{9,13},{10,... | collective-permute-start | bytes 98312 | tf_op jit(solution)/shard_map/ppermute | solution.py:12
  25.4 5.2 %collective-permute-start.3 = (f32[1,128,64]{1,2,0:T(8,128)S(1)}, f32[1,128,64]{1,2,0:T(8,128)S(1)}, u32[]{:S(2)}, u32[]{:S(2)}) collective-permute-start(f32[1,128,64]{1,2,0:T(8,128)S(1)} %bitcast.278), channel_id=1, source_target_pairs={{0,8},{1,9},{2,10},{3,11},{4,12},{5,13},{6,14},{7,15},{8,0},{9,1},... | collective-permute-start | bytes 98312 | tf_op jit(solution)/shard_map/ppermute | solution.py:12
  29.0 5.2 %collective-permute-start.7 = (f32[1,128,64]{1,2,0:T(8,128)S(1)}, f32[1,128,64]{1,2,0:T(8,128)S(1)}, u32[]{:S(2)}, u32[]{:S(2)}) collective-permute-start(f32[1,128,64]{1,2,0:T(8,128)S(1)} %bitcast.268), channel_id=1, source_target_pairs={{0,8},{1,9},{2,10},{3,11},{4,12},{5,13},{6,14},{7,15},{8,0},{9,1},... | collective-permute-start | bytes 98312 | tf_op jit(solution)/shard_map/ppermute | solution.py:12
  36.9 1.6 %copy-start.8 = (f32[3,256,256]{2,1,0:T(8,128)S(1)}, f32[3,256,256]{2,1,0:T(8,128)}, u32[]{:S(2)}) copy-start(f32[3,256,256]{2,1,0:T(8,128)} %param.15) | copy-start | bytes 2359300
  37.2 1.0 %copy-start.14 = (f32[3,256,128]{2,1,0:T(8,128)S(1)}, f32[3,256,128]{2,1,0:T(8,128)}, u32[]{:S(2)}) copy-start(f32[3,256,128]{2,1,0:T(8,128)} %param.16) | copy-start | bytes 1179652
  37.6 1.3 %copy-start.10 = (f32[3,256,256]{2,1,0:T(8,128)S(1)}, f32[3,256,256]{2,1,0:T(8,128)}, u32[]{:S(2)}) copy-start(f32[3,256,256]{2,1,0:T(8,128)} %param.14) | copy-start | bytes 2359300
  40.8 1.0 %copy-start.12 = (f32[4,256,128]{2,1,0:T(8,128)S(1)}, f32[4,256,128]{2,1,0:T(8,128)}, u32[]{:S(2)}) copy-start(f32[4,256,128]{2,1,0:T(8,128)} %param.13) | copy-start | bytes 1572868
  41.8 1.0 %copy-start.5 = (f32[4,128,256]{2,1,0:T(8,128)S(1)}, f32[4,128,256]{2,1,0:T(8,128)}, u32[]{:S(2)}) copy-start(f32[4,128,256]{2,1,0:T(8,128)} %copy-done.4) | copy-start | bytes 1572868
  42.9 1.2 %copy-start.6 = (f32[4,256,256]{2,1,0:T(8,128)S(1)}, f32[4,256,256]{2,1,0:T(8,128)}, u32[]{:S(2)}) copy-start(f32[4,256,256]{2,1,0:T(8,128)} %param.11) | copy-start | bytes 3145732
where the time goes:
time: 46.4 us; the launch traced here: 45.8 us
  matrix products  27.3 us (59%)
  starting transfers between devices  11.3 us (24%)
  local copies, waits for them, and re-layouts  4.45 us (10%)
  waiting for transfers between devices  2.34 us (5%)
    dot_general x40, matrix products, batched(): return jnp.einsum('nij,njr->nir', mats, vecs, precision=HIGH)  21.1 us
    ppermute x8, starting transfers between devices, swapped(): return lax.ppermute(value, axis, pairs)  11.3 us
    dot_general x18, matrix products, batched_t(): return jnp.einsum('nji,njr->nir', mats, vecs, precision=HIGH)  6.25 us
    unnamed x32, local copies, waits for them, and re-layouts  2.57 us
    ppermute x8, waiting for transfers between devices, swapped(): return lax.ppermute(value, axis, pairs)  2.34 us
    dot_general x3, local copies, waits for them, and re-layouts, batched_t(): return jnp.einsum('nji,njr->nir', mats, vecs, precision=HIGH)  1.22 us
  transfers between devices with their start and end apart: 8, of which 4 were waited for; matrix products, arithmetic and copies ran while one was open for 24% of the time, Pallas kernels for 0%

commit v1 on v0

v1 whole, which is shorter than its diff:
```python
import functools

import jax
import jax.numpy as jnp
from jax import lax
from jax.experimental import pallas as pl
from jax.experimental.pallas import tpu as pltpu
from jax.sharding import PartitionSpec as P

MESH = pl.DeviceIdType.MESH
F32, BF16 = jnp.float32, jnp.bfloat16
NN, NT, TN = ((1,), (0,)), ((1,), (1,)), ((0,), (0,))


def split(x):
    hi = x.astype(BF16)
    return hi, (x - hi.astype(F32)).astype(BF16)


def dot3(a, b, dims=NN):
    def one(x, y):
        return lax.dot_general(x, y, (dims, ((), ())), preferred_element_type=F32)

    return one(a[0], b[0]) + (one(a[0], b[1]) + one(a[1], b[0]))


def cat(*xs):
    return jnp.concatenate(xs, axis=1)


def plan(n):
    total = n.bit_length() - 1
    cuts = [0]
    while cuts[-1] < total:
        cuts.append(min(cuts[-1] + 2, total))
    if len(cuts) == 2:
        cuts = [0, total - 1, total]
    return list(zip(cuts[:-1], cuts[1:]))


def kernel(n, *refs):
    (rhs_h, lq_h, le_h, lw_h, nq_h, ne_h, nw_h, tq_h, te_h, tw_h, out_h,
     rhs, lq, le, lw, nq, ne, nw, tq, te, tw, out,
     ye, ud, red, sent0, sent1, full, part, spread, sendg, gath,
     mat_hi, mat_lo, dn, fin_hi, fin_lo,
     sem_in, sem_out, send_sem, recv_sem, gsend_sem, grecv_sem) = refs
    stages = plan(n)
    levels = n.bit_length() - 1
    s = stages[0][1]
    S = 2**s
    leaves = rhs.shape[0]
    K = lw.shape[2]
    R = rhs.shape[2]
    r = R // S
    me = lax.axis_index("leaf")
    pos = lax.rem(me, S)

    def side(level):
        return lax.rem(me // 2 ** (level - 1), 2)

    loads = {}
    count = 0

    def load(name, src, dst, i):
        nonlocal count
        copy = pltpu.make_async_copy(src.at[i], dst.at[i], sem_in.at[count])
        copy.start()
        loads[name, i] = copy
        count += 1

    for i in range(leaves):
        load("rhs", rhs_h, rhs, i)
        load("lq", lq_h, lq, i)
        load("le", le_h, le, i)
        load("lw", lw_h, lw, i)
    for i in range(leaves - 1):
        load("nq", nq_h, nq, i)
        load("ne", ne_h, ne, i)
        load("nw", nw_h, nw, i)
    for i in range(levels):
        load("tq", tq_h, tq, i)
        load("te", te_h, te, i)
        load("tw", tw_h, tw, i)

    messages = []
    for a, b in stages:
        for d in range(1, 2 ** (b - a)):
            messages.append((a, d))

    barrier = pltpu.get_barrier_semaphore()
    for a, d in messages:
        pl.semaphore_signal(
            barrier, inc=1, device_id={"leaf": me ^ (d << a)}, device_id_type=MESH
        )

    nodes = [(lq, le, lw, i, ("lq", "le", "lw")) for i in range(leaves)]
    nodes += [(nq, ne, nw, i, ("nq", "ne", "nw")) for i in range(leaves - 1)]

    def up(k, vecs):
        q, e, w, i, names = nodes[k]
        loads[names[0], i].wait()
        t = dot3(split(q[i]), split(vecs))
        loads[names[1], i].wait()
        loads[names[2], i].wait()
        both = dot3(split(e[i]), split(cat(t, w[i])))
        ye[k] = both
        return split(both[:, :R]), split(w[i])

    def solve(k):
        q, _, _, i, _ = nodes[k]
        ud[k] = dot3(split(q[i]), split(ye[k]), TN)

    def top(level):
        i = level - 1
        for name in ("tq", "te", "tw"):
            loads[name, i].wait()
        right = side(level) == 1
        q, w = tq[i], tw[i]
        if level == levels:
            rows = jnp.where(right, te[i, K:, :], te[i, :K, :])
            m = dot3(split(rows), split(q))
            height = K
        else:
            mine = jnp.where(right, q[:, K:], q[:, :K])
            z = cat(w, mine)
            if level == s:
                z = cat(z, jnp.where(right, q[:, :K], q[:, K:]))
            height = z.shape[1]
            ze = dot3(split(z), split(te[i]), TN)
            zs = split(ze)
            m = dot3(zs, split(q))
            dn[i, : height - K] = dot3(split(ze[K:]), split(w))
        own = jnp.where(right, m[:, K:], m[:, :K])
        sib = jnp.where(right, m[:, :K], m[:, K:])
        mat_hi[i, 0, :height], mat_lo[i, 0, :height] = split(own)
        mat_hi[i, 1, :height], mat_lo[i, 1, :height] = split(sib)
        return height

    def mat(level, which, low, high):
        i = level - 1
        return mat_hi[i, which, low:high], mat_lo[i, which, low:high]

    for k in range(leaves):
        loads["rhs", k].wait()
        y, w = up(k, rhs[k])
        red[k // 2, k % 2 * K : k % 2 * K + K] = dot3(w, y, TN)
    below, k = leaves, leaves
    heights = {}
    base = 0
    while below > 1:
        if below == 2:
            heights[1] = top(1)
        nxt = below // 2
        for j in range(nxt):
            y, w = up(k, red[base + j])
            if nxt > 1:
                red[base + nxt + j // 2, j % 2 * K : j % 2 * K + K] = dot3(w, y, TN)
            else:
                reduced = dot3(y, w, TN)
            k += 1
        base += nxt
        below = nxt

    pl.semaphore_wait(barrier, len(messages))

    def exchange(index, a, d, src, dst):
        copy = pltpu.make_async_remote_copy(
            src_ref=src,
            dst_ref=dst,
            send_sem=send_sem.at[index],
            recv_sem=recv_sem.at[index],
            device_id={"leaf": me ^ (d << a)},
            device_id_type=MESH,
        )
        copy.start()
        return copy

    u_top = {}
    copies = {}
    index = 0
    current = reduced
    for number, (a, b) in enumerate(stages):
        first = number == 0
        moved = current
        for l in range(a, b):
            if l > a:
                moved = dot3(split(moved), mat(l, 0, 0, K), NT)
            if first:
                sent0[l] = moved.reshape(S, r, K)
            else:
                sent1[l] = moved
            for d in range(2 ** (l - a), 2 ** (l - a + 1)):
                if first and l + 1 < s:
                    copies[a, d] = exchange(index, a, d, sent0.at[l], full.at[d])
                elif first:
                    block = lax.rem(me ^ d, S)
                    copies[a, d] = exchange(index, a, d, sent0.at[l, block], part.at[index])
                else:
                    copies[a, d] = exchange(index, a, d, sent1.at[l], part.at[index])
                index += 1
        if first:
            for l in range(2, levels + 1):
                if l <= stages[1][1]:
                    heights[l] = top(l)
            for k in range(leaves):
                solve(k)
        if number == 1 or len(stages) == 1:
            for l in range(stages[1][1] + 1, levels + 1):
                heights[l] = top(l)
            for k in range(leaves, 2 * leaves - 1):
                solve(k)
            k = 2 * leaves - 2
            u, d_ = ud[k, :, :R], ud[k, :, R:]
            for l in range(1, s):
                ds = split(d_)
                u = u - dot3(ds, split(u_top[l]), NT)
                d_ = -dot3(ds, split(dn[l - 1, :K]))
            ud[k] = cat(u, d_)
            count_here, start = 1, k
            while count_here < leaves:
                kids = start - 2 * count_here
                for j in range(2 * count_here):
                    half = j % 2 * K
                    both = split(ud[start + j // 2, half : half + K])
                    kid = ud[kids + j]
                    moved_ = dot3(split(kid[:, R:]), both)
                    ud[kids + j] = cat(kid[:, :R] - moved_[:, :R], -moved_[:, R:])
                start, count_here = kids, 2 * count_here
            for j in range(leaves):
                fin_hi[j], fin_lo[j] = split(ud[j, :, R:])
        if b == levels:
            m = None
            for l in range(levels - 1, s - 1, -1):
                lower = dn[l - 1, : heights[l] - K]
                step = mat(levels, 1, 0, K) if m is None else split(m)
                m = -dot3(split(lower), step)
            last = split(m)
        for l in range(a + 1, b + 1):
            group = range(2 ** (l - a - 1), 2 ** (l - a))
            if l == s:
                spread[...] = current.reshape(S, r, K)
                current = spread[pos]
            known = None
            if l < levels:
                h = heights[l]
                known = dot3(split(current), mat(l, 0, 0, h), NT)
            else:
                known = dot3(split(current), mat(l, 0, 0, K), NT)
                for low in range(levels - 1, s - 1, -1):
                    lower = split(dn[low - 1, : heights[low] - K])
                    known = u_top[low] - dot3(split(known), lower, NT)
            sib = None
            for d in group:
                copies[a, d].wait_recv()
                if first and l < s:
                    got = full[d].reshape(R, K)
                else:
                    got = part[messages.index((a, d))]
                sib = got if sib is None else sib + got
            if l < levels:
                both = known + dot3(split(sib), mat(l, 1, 0, h), NT)
                current = both[:, :K]
                u_top[l] = both[:, K:]
            else:
                answer = known + dot3(split(sib), last, NT)

    sendg[0] = answer[:, :K]
    sendg[1] = answer[:, K:]
    gcopies = []
    for d in range(S - 1, 0, -1):
        copy = pltpu.make_async_remote_copy(
            src_ref=sendg.at[1 if d >= S // 2 else 0],
            dst_ref=gath.at[pos],
            send_sem=gsend_sem.at[d],
            recv_sem=grecv_sem.at[d],
            device_id={"leaf": me ^ d},
            device_id_type=MESH,
        )
        copy.start()
        gcopies.append(copy)
    gath[pos] = answer[:, :K]
    for copy in gcopies:
        copy.wait_recv()
    g = split(gath[...].reshape(R, K))
    outs = []
    for j in range(leaves):
        out[j] = ud[j, :, :R] - dot3((fin_hi[j], fin_lo[j]), g, NT)
        copy = pltpu.make_async_copy(out.at[j], out_h.at[j], sem_out.at[j])
        copy.start()
        outs.append(copy)
    for copy in copies.values():
        copy.wait_send()
    for copy in gcopies:
        copy.wait_send()
    for copy in outs:
        copy.wait()


def body(n, *args):
    rhs, leaf_w, top_q = args[0], args[3], args[7]
    leaves, M, R = rhs.shape
    K = leaf_w.shape[2]
    levels = n.bit_length() - 1
    stages = plan(n)
    s = stages[0][1]
    S = 2**s
    r = R // S
    msgs = sum(2 ** (b - a) - 1 for a, b in stages)
    local = 2 * leaves - 1
    scratch = [pltpu.VMEM(x.shape, x.dtype) for x in args]
    scratch += [
        pltpu.VMEM((leaves, M, R), F32),
        pltpu.VMEM((local, M, R + K), F32),
        pltpu.VMEM((local, M, R + K), F32),
        pltpu.VMEM((leaves, 2 * K, R), F32),
        pltpu.VMEM((s, S, r, K), F32),
        pltpu.VMEM((levels, r, K), F32),
        pltpu.VMEM((S, S, r, K), F32),
        pltpu.VMEM((msgs, r, K), F32),
        pltpu.VMEM((S, r, K), F32),
        pltpu.VMEM((2, r, K), F32),
        pltpu.VMEM((S, r, K), F32),
        pltpu.VMEM((levels, 2, 3 * K, K), BF16),
        pltpu.VMEM((levels, 2, 3 * K, K), BF16),
        pltpu.VMEM((levels, 2 * K, K), F32),
        pltpu.VMEM((leaves, M, K), BF16),
        pltpu.VMEM((leaves, M, K), BF16),
        pltpu.SemaphoreType.DMA((4 * leaves + 3 * (leaves - 1) + 3 * levels,)),
        pltpu.SemaphoreType.DMA((leaves,)),
        pltpu.SemaphoreType.DMA((msgs,)),
        pltpu.SemaphoreType.DMA((msgs,)),
        pltpu.SemaphoreType.DMA((S,)),
        pltpu.SemaphoreType.DMA((S,)),
    ]
    return pl.pallas_call(
        functools.partial(kernel, n),
        out_shape=jax.ShapeDtypeStruct((leaves, M, R), F32),
        in_specs=[pl.BlockSpec(memory_space=pl.ANY)] * len(args),
        out_specs=pl.BlockSpec(memory_space=pl.ANY),
        scratch_shapes=scratch,
        compiler_params=pltpu.CompilerParams(collective_id=0, has_side_effects=True),
    )(*args)


def solution(mesh):
    spec = P(("freq", "leaf"), None, None)
    return jax.shard_map(
        functools.partial(body, mesh.shape["leaf"]),
        mesh=mesh,
        in_specs=(spec,) * 10,
        out_specs=spec,
        check_vma=False,
    )
```

time: 46.4 us -> 25.5 us (0.55)
  matrix products: 27.3 us -> 0 us
  Pallas kernels: 0 us -> 23.5 us
  starting transfers between devices: 11.3 us -> 0 us
  local copies, waits for them, and re-layouts: 4.45 us -> 1.87 us
  waiting for transfers between devices: 2.34 us -> 0 us
    dot_general x58 -> x0, matrix products: 27.3 us -> none  [the longest x40 21.1 us: batched(): return jnp.einsum('nij,njr->nir', mats, vecs, precision=HIGH)]
    pallas_call x0 -> x1, Pallas kernels: none -> 23.5 us  [body(): pl.pallas_call(functools.partial(kernel, n), out_shape=jax.ShapeDtypeStru...]
    ppermute x8 -> x0, starting transfers between devices: 11.3 us -> none  [swapped(): return lax.ppermute(value, axis, pairs)]
    ppermute x8 -> x0, waiting for transfers between devices: 2.34 us -> none  [swapped(): return lax.ppermute(value, axis, pairs)]
    dot_general x3 -> x0, local copies, waits for them, and re-layouts: 1.22 us -> none  [batched_t(): return jnp.einsum('nji,njr->nir', mats, vecs, precision=HIGH)]
    unnamed x32 -> x1, local copies, waits for them, and re-layouts: 2.57 us -> 1.87 us
    slice x1 -> x0, local copies, waits for them, and re-layouts: 0.65 us -> none  [body(): first = tree_sweep(reduced[:, :, :half], top_q, top_e, top_w, width)]
  transfers between devices with their start and end apart: 8 -> 0, of which waited for: 4 -> 0; matrix products, arithmetic and copies ran while one was open for 24% -> 0% of each run, Pallas kernels for 0% -> 0%
where the time goes in v1:
time: 25.5 us; the launch traced here: 25.3 us
  Pallas kernels  23.5 us (92%)
  local copies, waits for them, and re-layouts  1.87 us (7%)
    pallas_call x1, Pallas kernels, body(): pl.pallas_call(functools.partial(kernel, n), out_shape=jax.ShapeDtypeStru...  23.5 us
    unnamed x1, local copies, waits for them, and re-layouts  1.87 us

profile of v1, /device:TPU:0, one launch (start us, length us, event | category | flops | bytes accessed | tf_op | source)
XLA Modules:
  0.0 25.3 jit_solution(17869434761785514802)
XLA Ops:
  0.0 23.5 %shard_map.100 = f32[4,256,128]{2,1,0:T(8,128)} custom-call(f32[4,256,128]{2,1,0:T(8,128)} %refs_0_.1, f32[4,256,256]{2,1,0:T(8,128)} %refs_1_.1, f32[4,256,256]{2,1,0:T(8,128)} %refs_2_.1, f32[4,256,128]{2,1,0:T(8,128)} %refs_3_.1, f32[3,256,256]{2,1,0:T(8,128)} %refs_4_.1, f32[3,256,256]{2,1,0:T(8,128)} %refs_5_.1, f32[3,256,128]{2,1,0:T(8,128)} %refs_6_.1, ...), custom_call_target="tpu_custom_call" | custom-call | tf_op jit(solution)/shard_map/pallas_call | solution.py:335
  23.5 1.9 %copy.12 = f32[4,256,128]{2,1,0:T(8,128)} copy(f32[4,256,128]{2,1,0:T(8,128)} %shard_map.100) | data formatting | bytes 1048576

commit v2 on v1

--- a/solution.py
+++ b/solution.py
@@ -41,7 +41,7 @@
 def kernel(n, *refs):
     (rhs_h, lq_h, le_h, lw_h, nq_h, ne_h, nw_h, tq_h, te_h, tw_h, out_h,
      rhs, lq, le, lw, nq, ne, nw, tq, te, tw, out,
-     ye, ud, red, sent0, sent1, full, part, spread, sendg, gath,
+     ye, ud, stacked, up_hi, up_lo, sent0, sent1, full, part, spread, sendg, gath,
      mat_hi, mat_lo, dn, fin_hi, fin_lo,
      sem_in, sem_out, send_sem, recv_sem, gsend_sem, grecv_sem) = refs
     stages = plan(n)
@@ -68,15 +68,16 @@
         loads[name, i] = copy
         count += 1
 
+    for i in range(leaves - 1):
+        load("nw", nw_h, nw, i)
+        load("ne", ne_h, ne, i)
+        load("nq", nq_h, nq, i)
     for i in range(leaves):
         load("rhs", rhs_h, rhs, i)
         load("lq", lq_h, lq, i)
+    for i in range(leaves):
+        load("lw", lw_h, lw, i)
         load("le", le_h, le, i)
-        load("lw", lw_h, lw, i)
-    for i in range(leaves - 1):
-        load("nq", nq_h, nq, i)
-        load("ne", ne_h, ne, i)
-        load("nw", nw_h, nw, i)
     for i in range(levels):
         load("tq", tq_h, tq, i)
         load("te", te_h, te, i)
@@ -93,22 +94,21 @@
             barrier, inc=1, device_id={"leaf": me ^ (d << a)}, device_id_type=MESH
         )
 
-    nodes = [(lq, le, lw, i, ("lq", "le", "lw")) for i in range(leaves)]
-    nodes += [(nq, ne, nw, i, ("nq", "ne", "nw")) for i in range(leaves - 1)]
-
-    def up(k, vecs):
-        q, e, w, i, names = nodes[k]
-        loads[names[0], i].wait()
-        t = dot3(split(q[i]), split(vecs))
-        loads[names[1], i].wait()
-        loads[names[2], i].wait()
-        both = dot3(split(e[i]), split(cat(t, w[i])))
-        ye[k] = both
-        return split(both[:, :R]), split(w[i])
+    def factors(k):
+        return (lq, le, lw, k) if k < leaves else (nq, ne, nw, k - leaves)
+
+    def values(k, t):
+        _, e, w, i = factors(k)
+        ye[k] = dot3(split(jnp.concatenate([t, w[i].T], axis=0)), split(e[i]), NT)
 
     def solve(k):
-        q, _, _, i, _ = nodes[k]
-        ud[k] = dot3(split(q[i]), split(ye[k]), TN)
+        q, _, _, i = factors(k)
+        ud[k] = dot3(split(ye[k]), split(q[i]))
+
+    def node(k):
+        i = k - leaves
+        values(k, dot3(split(stacked[i]), split(nq[i]), NT))
+        solve(k)
 
     def top(level):
         i = level - 1
@@ -140,26 +140,32 @@
         i = level - 1
         return mat_hi[i, which, low:high], mat_lo[i, which, low:high]
 
-    for k in range(leaves):
-        loads["rhs", k].wait()
-        y, w = up(k, rhs[k])
-        red[k // 2, k % 2 * K : k % 2 * K + K] = dot3(w, y, TN)
-    below, k = leaves, leaves
-    heights = {}
-    base = 0
-    while below > 1:
-        if below == 2:
-            heights[1] = top(1)
-        nxt = below // 2
-        for j in range(nxt):
-            y, w = up(k, red[base + j])
-            if nxt > 1:
-                red[base + nxt + j // 2, j % 2 * K : j % 2 * K + K] = dot3(w, y, TN)
-            else:
-                reduced = dot3(y, w, TN)
+    for i in range(leaves - 1):
+        for name in ("nw", "ne", "nq"):
+            loads[name, i].wait()
+    ze = [dot3(split(nw[i].T), split(ne[i])) for i in range(leaves - 1)]
+    for i in range(leaves - 1):
+        up_hi[i], up_lo[i] = split(dot3(split(ze[i]), split(nq[i])))
+    for i in range(leaves):
+        loads["rhs", i].wait()
+        loads["lq", i].wait()
+    ts = [dot3(split(rhs[i].T), split(lq[i]), NT) for i in range(leaves)]
+    for i in range(leaves):
+        loads["lw", i].wait()
+        loads["le", i].wait()
+    for i in range(leaves):
+        values(i, ts[i])
+    reduced = [dot3(split(ye[i, :R]), split(lw[i])) for i in range(leaves)]
+    heights = {1: top(1)}
+    k = 0
+    while len(reduced) > 1:
+        above = []
+        for j in range(len(reduced) // 2):
+            stacked[k] = cat(reduced[2 * j], reduced[2 * j + 1])
+            above.append(dot3(split(stacked[k]), (up_hi[k], up_lo[k]), NT))
             k += 1
-        base += nxt
-        below = nxt
+        reduced = above
+    reduced = reduced[0]
 
     pl.semaphore_wait(barrier, len(messages))
 
@@ -199,35 +205,33 @@
                     copies[a, d] = exchange(index, a, d, sent1.at[l], part.at[index])
                 index += 1
         if first:
-            for l in range(2, levels + 1):
-                if l <= stages[1][1]:
-                    heights[l] = top(l)
+            for l in range(2, stages[1][1]):
+                heights[l] = top(l)
+        if number == 1:
+            for l in range(stages[1][1], levels + 1):
+                heights[l] = top(l)
             for k in range(leaves):
                 solve(k)
-        if number == 1 or len(stages) == 1:
-            for l in range(stages[1][1] + 1, levels + 1):
-                heights[l] = top(l)
             for k in range(leaves, 2 * leaves - 1):
-                solve(k)
+                node(k)
             k = 2 * leaves - 2
-            u, d_ = ud[k, :, :R], ud[k, :, R:]
             for l in range(1, s):
-                ds = split(d_)
-                u = u - dot3(ds, split(u_top[l]), NT)
-                d_ = -dot3(ds, split(dn[l - 1, :K]))
-            ud[k] = cat(u, d_)
+                ds = split(ud[k, R:])
+                ud[k, :R] = ud[k, :R] - dot3(split(u_top[l]), ds)
+                ud[k, R:] = -dot3(split(dn[l - 1, :K]), ds, TN)
             count_here, start = 1, k
             while count_here < leaves:
                 kids = start - 2 * count_here
                 for j in range(2 * count_here):
                     half = j % 2 * K
-                    both = split(ud[start + j // 2, half : half + K])
-                    kid = ud[kids + j]
-                    moved_ = dot3(split(kid[:, R:]), both)
-                    ud[kids + j] = cat(kid[:, :R] - moved_[:, :R], -moved_[:, R:])
+                    both = split(ud[start + j // 2, :, half : half + K])
+                    shift = dot3(both, split(ud[kids + j, R:]))
+                    ud[kids + j, :R] = ud[kids + j, :R] - shift[:R]
+                    ud[kids + j, R:] = -shift[R:]
                 start, count_here = kids, 2 * count_here
             for j in range(leaves):
-                fin_hi[j], fin_lo[j] = split(ud[j, :, R:])
+                fin_hi[j], fin_lo[j] = split(ud[j, R:].T)
+                out[j] = ud[j, :R].T
         if b == levels:
             m = None
             for l in range(levels - 1, s - 1, -1):
@@ -284,7 +288,7 @@
     g = split(gath[...].reshape(R, K))
     outs = []
     for j in range(leaves):
-        out[j] = ud[j, :, :R] - dot3((fin_hi[j], fin_lo[j]), g, NT)
+        out[j] = out[j] - dot3((fin_hi[j], fin_lo[j]), g, NT)
         copy = pltpu.make_async_copy(out.at[j], out_h.at[j], sem_out.at[j])
         copy.start()
         outs.append(copy)
@@ -310,9 +314,11 @@
     scratch = [pltpu.VMEM(x.shape, x.dtype) for x in args]
     scratch += [
         pltpu.VMEM((leaves, M, R), F32),
-        pltpu.VMEM((local, M, R + K), F32),
-        pltpu.VMEM((local, M, R + K), F32),
-        pltpu.VMEM((leaves, 2 * K, R), F32),
+        pltpu.VMEM((local, R + K, M), F32),
+        pltpu.VMEM((local, R + K, M), F32),
+        pltpu.VMEM((leaves - 1, R, M), F32),
+        pltpu.VMEM((leaves - 1, K, M), BF16),
+        pltpu.VMEM((leaves - 1, K, M), BF16),
         pltpu.VMEM((s, S, r, K), F32),
         pltpu.VMEM((levels, r, K), F32),
         pltpu.VMEM((S, S, r, K), F32),

time: 25.5 us -> 21.9 us (0.86)
  Pallas kernels: 23.5 us -> 19.9 us
    pallas_call x1, Pallas kernels: 23.5 us -> 19.9 us  [body(): pl.pallas_call(functools.partial(kernel, n), out_shape=jax.ShapeDtypeStru...]
where the time goes in v2:
time: 21.9 us; the launch traced here: 21.7 us
  Pallas kernels  19.9 us (91%)
  local copies, waits for them, and re-layouts  1.87 us (9%)
    pallas_call x1, Pallas kernels, body(): pl.pallas_call(functools.partial(kernel, n), out_shape=jax.ShapeDtypeStru...  19.9 us
    unnamed x1, local copies, waits for them, and re-layouts  1.87 us

profile of v2, /device:TPU:0, one launch (start us, length us, event | category | flops | bytes accessed | tf_op | source)
XLA Modules:
  0.0 21.7 jit_solution(1890097005139997529)
XLA Ops:
  0.0 19.9 %shard_map.100 = f32[4,256,128]{2,1,0:T(8,128)} custom-call(f32[4,256,128]{2,1,0:T(8,128)} %refs_0_.1, f32[4,256,256]{2,1,0:T(8,128)} %refs_1_.1, f32[4,256,256]{2,1,0:T(8,128)} %refs_2_.1, f32[4,256,128]{2,1,0:T(8,128)} %refs_3_.1, f32[3,256,256]{2,1,0:T(8,128)} %refs_4_.1, f32[3,256,256]{2,1,0:T(8,128)} %refs_5_.1, f32[3,256,128]{2,1,0:T(8,128)} %refs_6_.1, ...), custom_call_target="tpu_custom_call" | custom-call | tf_op jit(solution)/shard_map/pallas_call | solution.py:341
  19.9 1.9 %copy.12 = f32[4,256,128]{2,1,0:T(8,128)} copy(f32[4,256,128]{2,1,0:T(8,128)} %shard_map.100) | data formatting | bytes 1048576

commit v3 on v2

--- a/solution.py
+++ b/solution.py
@@ -39,11 +39,11 @@
 
 
 def kernel(n, *refs):
-    (rhs_h, lq_h, le_h, lw_h, nq_h, ne_h, nw_h, tq_h, te_h, tw_h, out_h,
-     rhs, lq, le, lw, nq, ne, nw, tq, te, tw, out,
+    (rhs_h, lq_h, le_h, lw_h, nq_h, ne_h, nw_h, tq_h, te_h, tw_h, out, fin_hi, fin_lo, g_out,
+     rhs, lq, le, lw, nq, ne, nw, tq, te, tw,
      ye, ud, stacked, up_hi, up_lo, sent0, sent1, full, part, spread, sendg, gath,
-     mat_hi, mat_lo, dn, fin_hi, fin_lo,
-     sem_in, sem_out, send_sem, recv_sem, gsend_sem, grecv_sem) = refs
+     mat_hi, mat_lo, dn,
+     sem_in, send_sem, recv_sem, gsend_sem, grecv_sem) = refs
     stages = plan(n)
     levels = n.bit_length() - 1
     s = stages[0][1]
@@ -285,18 +285,21 @@
     gath[pos] = answer[:, :K]
     for copy in gcopies:
         copy.wait_recv()
-    g = split(gath[...].reshape(R, K))
-    outs = []
-    for j in range(leaves):
-        out[j] = out[j] - dot3((fin_hi[j], fin_lo[j]), g, NT)
-        copy = pltpu.make_async_copy(out.at[j], out_h.at[j], sem_out.at[j])
-        copy.start()
-        outs.append(copy)
+    g_out[...] = gath[...].reshape(R, K)
     for copy in copies.values():
         copy.wait_send()
     for copy in gcopies:
         copy.wait_send()
-    for copy in outs:
+
+
+def finish(base, fin_hi, fin_lo, g_in, out_h, out, sem):
+    g = split(g_in[...])
+    copies = []
+    for j in range(base.shape[0]):
+        out[j] = base[j] - dot3((fin_hi[j], fin_lo[j]), g, NT)
+        copies.append(pltpu.make_async_copy(out.at[j], out_h.at[j], sem.at[j]))
+        copies[-1].start()
+    for copy in copies:
         copy.wait()
 
 
@@ -313,7 +316,6 @@
     local = 2 * leaves - 1
     scratch = [pltpu.VMEM(x.shape, x.dtype) for x in args]
     scratch += [
-        pltpu.VMEM((leaves, M, R), F32),
         pltpu.VMEM((local, R + K, M), F32),
         pltpu.VMEM((local, R + K, M), F32),
         pltpu.VMEM((leaves - 1, R, M), F32),
@@ -329,23 +331,40 @@
         pltpu.VMEM((levels, 2, 3 * K, K), BF16),
         pltpu.VMEM((levels, 2, 3 * K, K), BF16),
         pltpu.VMEM((levels, 2 * K, K), F32),
-        pltpu.VMEM((leaves, M, K), BF16),
-        pltpu.VMEM((leaves, M, K), BF16),
         pltpu.SemaphoreType.DMA((4 * leaves + 3 * (leaves - 1) + 3 * levels,)),
-        pltpu.SemaphoreType.DMA((leaves,)),
         pltpu.SemaphoreType.DMA((msgs,)),
         pltpu.SemaphoreType.DMA((msgs,)),
         pltpu.SemaphoreType.DMA((S,)),
         pltpu.SemaphoreType.DMA((S,)),
     ]
+    vmem = pl.BlockSpec(memory_space=pltpu.VMEM)
+    anywhere = pl.BlockSpec(memory_space=pl.ANY)
+    parts = pl.pallas_call(
+        functools.partial(kernel, n),
+        out_shape=(
+            pltpu.VMEM((leaves, M, R), F32),
+            pltpu.VMEM((leaves, M, K), BF16),
+            pltpu.VMEM((leaves, M, K), BF16),
+            pltpu.VMEM((R, K), F32),
+        ),
+        in_specs=[anywhere] * len(args),
+        out_specs=(vmem,) * 4,
+        scratch_shapes=scratch,
+        compiler_params=pltpu.CompilerParams(
+            collective_id=0, has_side_effects=True
+        ),
+    )(*args)
     return pl.pallas_call(
-        functools.partial(kernel, n),
+        finish,
         out_shape=jax.ShapeDtypeStruct((leaves, M, R), F32),
-        in_specs=[pl.BlockSpec(memory_space=pl.ANY)] * len(args),
-        out_specs=pl.BlockSpec(memory_space=pl.ANY),
-        scratch_shapes=scratch,
-        compiler_params=pltpu.CompilerParams(collective_id=0, has_side_effects=True),
-    )(*args)
+        in_specs=[vmem] * 4,
+        out_specs=anywhere,
+        scratch_shapes=[
+            pltpu.VMEM((leaves, M, R), F32),
+            pltpu.SemaphoreType.DMA((leaves,)),
+        ],
+        compiler_params=pltpu.CompilerParams(vmem_limit_bytes=8 * 2**20),
+    )(*parts)
 
 
 def solution(mesh):

time: 21.9 us -> 20 us (0.913)
  local copies, waits for them, and re-layouts: 1.87 us -> 0 us
    unnamed x1 -> x0, local copies, waits for them, and re-layouts: 1.87 us -> none
    pallas_call x1 -> x2, Pallas kernels: 19.9 us -> 19.9 us  [the longest x1 18.8 us: body(): pl.pallas_call(functools.partial(kernel, n), out_shape=(pltpu.VMEM((leave...]
where the time goes in v3:
time: 20 us; the launch traced here: 19.9 us
  Pallas kernels  19.9 us (99%)
    pallas_call x1, Pallas kernels, body(): pl.pallas_call(functools.partial(kernel, n), out_shape=(pltpu.VMEM((leave...  18.8 us
    pallas_call x1, Pallas kernels, body(): pl.pallas_call(finish, out_shape=jax.ShapeDtypeStruct((leaves, M, R), F32...  1.12 us

profile of v3, /device:TPU:0, one launch (start us, length us, event | category | flops | bytes accessed | tf_op | source)
XLA Modules:
  0.0 19.9 jit_solution(13290528007532265094)
XLA Ops:
  0.0 18.8 %shard_map.100 = (f32[4,256,128]{2,1,0:T(8,128)S(1)}, bf16[4,256,128]{2,1,0:T(8,128)(2,1)S(1)}, bf16[4,256,128]{2,1,0:T(8,128)(2,1)S(1)}, f32[128,128]{1,0:T(8,128)S(1)}) custom-call(f32[4,256,128]{2,1,0:T(8,128)} %refs_0_.1, f32[4,256,256]{2,1,0:T(8,128)} %refs_1_.1, f32[4,256,256]{2,1,0:T(8,128)} %refs_2_.1, f32[4,256,128]{2,1,0:T(8,128)} %refs_3_.1, ...), custom_call_target="tpu_custom_call" | custom-call | tf_op jit(solution)/shard_map/pallas_call | solution.py:342
  18.8 1.1 %shard_map.101 = f32[4,256,128]{2,1,0:T(8,128)} custom-call(f32[4,256,128]{2,1,0:T(8,128)S(1)} %get-tuple-element.9.base, bf16[4,256,128]{2,1,0:T(8,128)(2,1)S(1)} %get-tuple-element.10.fin_hi, bf16[4,256,128]{2,1,0:T(8,128)(2,1)S(1)} %get-tuple-element.11.fin_lo, f32[128,128]{1,0:T(8,128)S(1)} %get-tuple-element.12.g_in), custom_call_target="tpu_custom_call" | custom-call | tf_op jit(solution)/shard_map/pallas_call | solution.py:357
